TPU v7x, 32 devices: a whole 2x2x4 slice. The times are simulated.
32 devices in a mesh: batch: 4 (over y, x), cols: 8 (over z, core).
Axes of the slice: x: 2, y: 2, z: 4, core: 2. Of those that a mesh axis runs over, the one named last changes fastest.
Arguments:
- grad_query: float32 [4, 2048, 2048], P('batch', None, 'cols'), may hold values from -0.875 to 0.875
- grad_key: float32 [4, 2048, 2048], P('batch', None, 'cols'), may hold values from -0.875 to 0.875
- grad_value: float32 [4, 2048, 2048], P('batch', None, 'cols'), may hold values from -0.875 to 0.875
- grad_mixed: float32 [4, 2048, 2048], P('batch', 'cols'), may hold values from -0.875 to 0.875
- grad_norm: float32 [4, 2048], P('batch'), may hold values from -8 to 8
- grad_bias: float32 [4, 2048], P('batch'), may hold values from -8 to 8
- weight_query: float32 [2048, 2048], P('batch', 'cols'), may hold values from -0.1875 to 0.1875
- weight_key: float32 [2048, 2048], P('batch', 'cols'), may hold values from -0.1875 to 0.1875
- weight_value: float32 [2048, 2048], P('batch', 'cols'), may hold values from -0.1875 to 0.1875
- weight_mixed: float32 [2048, 2048], P('cols', 'batch'), may hold values from -0.1875 to 0.1875
- weight_norm: float32 [2048], P('batch'), may hold values from 0.25 to 1.75
- weight_bias: float32 [2048], P('batch'), may hold values from -3 to 3
Outputs:
- copy_query: bfloat16 [2048, 2048], P(None, 'cols')
- copy_key: bfloat16 [2048, 2048], P(None, 'cols')
- copy_value: bfloat16 [2048, 2048], P(None, 'cols')
- copy_mixed: bfloat16 [2048, 2048], P('cols')
- copy_norm: bfloat16 [2048], replicated
- copy_bias: bfloat16 [2048], replicated
- new_query: float32 [2048, 2048], P('batch', 'cols')
- new_key: float32 [2048, 2048], P('batch', 'cols')
- new_value: float32 [2048, 2048], P('batch', 'cols')
- new_mixed: float32 [2048, 2048], P('cols', 'batch')
- new_norm: float32 [2048], P('batch')
- new_bias: float32 [2048], P('batch')
All inputs are finite; a program needn't handle non-finite values.
Results may differ from a plain program's by a relative error of at most 0.0004.
Values may be sent and summed in bfloat16 or wider, within the bound.
A program may use at most 64 MiB of HBM per device.

v0:
```python
import jax
import jax.numpy as jnp
from jax import lax
from jax.sharding import PartitionSpec as P

learn_rate = 0.4


def per_device(
    grad_query,
    grad_key,
    grad_value,
    grad_mixed,
    grad_norm,
    grad_bias,
    weight_query,
    weight_key,
    weight_value,
    weight_mixed,
    weight_norm,
    weight_bias,
):
    mean_query, mean_key, mean_value, mean_mixed, mean_norm, mean_bias = (
        lax.psum_scatter(grad_query[0], "batch", scatter_dimension=0, tiled=True),
        lax.psum_scatter(grad_key[0], "batch", scatter_dimension=0, tiled=True),
        lax.psum_scatter(grad_value[0], "batch", scatter_dimension=0, tiled=True),
        lax.psum_scatter(grad_mixed[0], "batch", scatter_dimension=1, tiled=True),
        lax.psum_scatter(grad_norm[0], "batch", scatter_dimension=0, tiled=True),
        lax.psum_scatter(grad_bias[0], "batch", scatter_dimension=0, tiled=True),
    )
    mean_rate = lax.axis_size("batch") ** (-0.5)
    mean_query = mean_query * mean_rate
    mean_key = mean_key * mean_rate
    mean_value = mean_value * mean_rate
    mean_mixed = mean_mixed * mean_rate
    mean_norm = mean_norm * mean_rate
    mean_bias = mean_bias * mean_rate
    (
        own_query,
        own_key,
        own_value,
        own_mixed,
        slope_query_norm,
        slope_key_norm,
        slope_value_norm,
        slope_mixed_norm,
    ) = lax.psum(
        (
            jnp.sum(weight_query * weight_query, axis=1, keepdims=True),
            jnp.sum(weight_key * weight_key, axis=1, keepdims=True),
            jnp.sum(weight_value * weight_value, axis=1, keepdims=True),
            jnp.sum(weight_mixed * weight_mixed, axis=0, keepdims=True),
            jnp.sum(mean_query * mean_query, axis=1, keepdims=True),
            jnp.sum(mean_key * mean_key, axis=1, keepdims=True),
            jnp.sum(mean_value * mean_value, axis=1, keepdims=True),
            jnp.sum(mean_mixed * mean_mixed, axis=0, keepdims=True),
        ),
        "cols",
    )
    mean_query = mean_query * (jnp.sqrt(own_query) * lax.rsqrt(slope_query_norm + 1e-06))
    mean_key = mean_key * (jnp.sqrt(own_key) * lax.rsqrt(slope_key_norm + 1e-06))
    mean_value = mean_value * (jnp.sqrt(own_value) * lax.rsqrt(slope_value_norm + 1e-06))
    mean_mixed = mean_mixed * (jnp.sqrt(own_mixed) * lax.rsqrt(slope_mixed_norm + 1e-06))
    new_query = weight_query - learn_rate * mean_query
    new_key = weight_key - learn_rate * mean_key
    new_value = weight_value - learn_rate * mean_value
    new_mixed = weight_mixed - learn_rate * mean_mixed
    new_norm = weight_norm - learn_rate * mean_norm
    new_bias = weight_bias - learn_rate * mean_bias
    copy_query, copy_key, copy_value, copy_mixed, copy_norm, copy_bias = (
        lax.all_gather(new_query.astype(jnp.bfloat16), "batch", axis=0, tiled=True),
        lax.all_gather(new_key.astype(jnp.bfloat16), "batch", axis=0, tiled=True),
        lax.all_gather(new_value.astype(jnp.bfloat16), "batch", axis=0, tiled=True),
        lax.all_gather(new_mixed.astype(jnp.bfloat16), "batch", axis=1, tiled=True),
        lax.all_gather(new_norm.astype(jnp.bfloat16), "batch", axis=0, tiled=True),
        lax.all_gather(new_bias.astype(jnp.bfloat16), "batch", axis=0, tiled=True),
    )
    return (
        copy_query,
        copy_key,
        copy_value,
        copy_mixed,
        copy_norm,
        copy_bias,
        new_query,
        new_key,
        new_value,
        new_mixed,
        new_norm,
        new_bias,
    )


def solution(mesh):
    in_specs = (
        P("batch", None, "cols"),
        P("batch", None, "cols"),
        P("batch", None, "cols"),
        P("batch", "cols", None),
        P("batch", None),
        P("batch", None),
        P("batch", "cols"),
        P("batch", "cols"),
        P("batch", "cols"),
        P("cols", "batch"),
        P("batch"),
        P("batch"),
    )
    out_specs = (
        P(None, "cols"),
        P(None, "cols"),
        P(None, "cols"),
        P("cols", None),
        P(),
        P(),
        P("batch", "cols"),
        P("batch", "cols"),
        P("batch", "cols"),
        P("cols", "batch"),
        P("batch"),
        P("batch"),
    )
    return jax.shard_map(
        per_device, mesh=mesh, in_specs=in_specs, out_specs=out_specs, check_vma=False
    )
```

profile of v0, /device:TPU:0, one launch (start us, length us, event | category | flops | bytes accessed | tf_op | source)
XLA Modules:
  0.0 317.6 jit_solution(17329682381888189830)
XLA Ops:
  8.0 0.7 reduce-scatter.11.cloned.1.call-update
  10.8 38.1 %reduce-scatter.9.cloned.1.call-done = f32[512,256]{1,0:T(8,128)} async-done(((f32[2048,256]{1,0:T(8,128)}), f32[512,256]{1,0:T(8,128)}) %reduce-scatter.9.cloned.1.call-update) | async-done | bytes 524304 | tf_op jit(solution)/shard_map/reduce_scatter | solution.py:26
  48.9 1.3 multiply_reduce_fusion.2
  50.2 36.9 %reduce-scatter.11.cloned.1.call-done = f32[256,512]{1,0:T(8,128)} async-done(((f32[256,2048]{1,0:T(8,128)}), f32[256,512]{1,0:T(8,128)}) %reduce-scatter.11.cloned.1.call-update) | async-done | bytes 524304 | tf_op jit(solution)/shard_map/reduce_scatter | solution.py:27
  87.1 1.1 multiply_reduce_fusion
  88.2 37.1 %reduce-scatter.5.cloned.1.call-done = f32[512,256]{1,0:T(8,128)} async-done(((f32[2048,256]{1,0:T(8,128)}), f32[512,256]{1,0:T(8,128)}) %reduce-scatter.5.cloned.1.call-update) | async-done | bytes 524304 | tf_op jit(solution)/shard_map/reduce_scatter | solution.py:24
  125.3 1.2 multiply_reduce_fusion.6
  126.5 36.8 %reduce-scatter.7.cloned.1.call-done = f32[512,256]{1,0:T(8,128)} async-done(((f32[2048,256]{1,0:T(8,128)}), f32[512,256]{1,0:T(8,128)}) %reduce-scatter.7.cloned.1.call-update) | async-done | bytes 524304 | tf_op jit(solution)/shard_map/reduce_scatter | solution.py:25
  163.3 1.2 multiply_reduce_fusion.4
  164.5 28.3 %all-reduce.2 = (f32[512,1]{0,1:T(1,128)S(1)}, f32[512,1]{0,1:T(1,128)S(1)}, f32[512,1]{0,1:T(1,128)S(1)}, f32[512,1]{0,1:T(1,128)S(1)}, f32[512,1]{0,1:T(1,128)...) all-reduce(f32[512,1]{0,1:T(1,128)S(1)} %bitcast.35, ...), channel_id=1, replica_groups=mesh['batch'=4,'cols'=8] {'cols'}, use_global_device_ids=true, to_apply=%region_4.0 | all-reduce | flops 4096 | bytes 32768 | tf_op jit(solution)/shard_map/psum | solution.py:47
  192.9 2.1 fusion.8
  195.1 1.0 fusion.7
  196.3 1.0 fusion.6
  197.4 1.0 fusion.9
  199.7 15.2 %all-reduce.3 = (f32[2048]{0:T(1024)S(1)}, f32[2048]{0:T(1024)S(1)}) all-reduce(f32[2048]{0:T(1024)S(1)} %bitcast.37, f32[2048]{0:T(1024)S(1)} %bitcast.38), channel_id=6, replica_groups=mesh['batch'=4,'cols'=8] {'batch'}, use_global_device_ids=true, to_apply=%region_20.0.clone | all-reduce | flops 4096 | bytes 32768
  215.6 8.1 %all-gather = bf16[4,1,512]{2,1,0:T(2,128)(2,1)S(1)} all-gather(bf16[1,1,512]{2,1,0:T(2,128)(2,1)S(1)} %reshape.32), channel_id=1, replica_groups=mesh['batch'=4,'cols'=8] {'batch'}, dimensions={0}, use_global_device_ids=true | all-gather | bytes 5120 | tf_op jit(solution)/shard_map/all_gather | solution.py:75
  224.3 7.1 %all-gather.1 = bf16[4,1,512]{2,1,0:T(2,128)(2,1)S(1)} all-gather(bf16[1,1,512]{2,1,0:T(2,128)(2,1)S(1)} %reshape.34), channel_id=1, replica_groups=mesh['batch'=4,'cols'=8] {'batch'}, dimensions={0}, use_global_device_ids=true | all-gather | bytes 5120 | tf_op jit(solution)/shard_map/all_gather | solution.py:76
  232.0 15.8 %all-gather.11.cloned.1.call-done = bf16[2048,256]{1,0:T(8,128)(2,1)} async-done(((bf16[512,256]{1,0:T(8,128)(2,1)}), bf16[2048,256]{1,0:T(8,128)(2,1)}) %all-gather.11.cloned.1.call-update) | async-done | bytes 1048592 | tf_op jit(solution)/shard_map/all_gather | solution.py:73
  247.8 28.8 %all-gather.13.cloned.1.call-done = bf16[256,2048]{1,0:T(8,128)(2,1)} async-done(((bf16[256,512]{1,0:T(8,128)(2,1)}), bf16[256,2048]{1,0:T(8,128)(2,1)}) %all-gather.13.cloned.1.call-update) | async-done | bytes 1048592 | tf_op jit(solution)/shard_map/all_gather | solution.py:74
  276.6 28.9 %all-gather.7.cloned.1.call-done = bf16[2048,256]{1,0:T(8,128)(2,1)} async-done(((bf16[512,256]{1,0:T(8,128)(2,1)}), bf16[2048,256]{1,0:T(8,128)(2,1)}) %all-gather.7.cloned.1.call-update) | async-done | bytes 1048592 | tf_op jit(solution)/shard_map/all_gather | solution.py:71
  305.5 2.4 copy.30
  307.9 1.0 copy.31
  308.8 1.0 copy.32
  309.8 1.0 copy.33
  (61 shorter events, 5.6 us)
Async XLA Ops:
  7.2 41.7 %reduce-scatter.9.cloned.1.call-start = ((), (), s32[]{:S(2)}) async-start(), calls=%async_computation.8 | async-start | bytes 2621440 | tf_op jit(solution)/shard_map/reduce_scatter | solution.py:26
  7.9 79.2 %reduce-scatter.11.cloned.1.call-start = ((), (), s32[]{:S(2)}) async-start(), calls=%async_computation.10 | async-start | bytes 2621440 | tf_op jit(solution)/shard_map/reduce_scatter | solution.py:27
  8.7 116.6 %reduce-scatter.5.cloned.1.call-start = ((), (), s32[]{:S(2)}) async-start(), calls=%async_computation.4 | async-start | bytes 2621440 | tf_op jit(solution)/shard_map/reduce_scatter | solution.py:24
  8.7 1.3 copy-start.3
  8.7 1.5 copy-start.2
  9.4 1.1 copy-start
  9.4 1.3 copy-start.1
  9.4 153.9 %reduce-scatter.7.cloned.1.call-start = ((), (), s32[]{:S(2)}) async-start(), calls=%async_computation.6 | async-start | bytes 2621440 | tf_op jit(solution)/shard_map/reduce_scatter | solution.py:25
  10.0 222.0 %all-gather.9.cloned.1.call-start = ((), (), s32[]{:S(2)}) async-start(), calls=%async_computation.7 | async-start | bytes 1310720 | tf_op jit(solution)/shard_map/all_gather | solution.py:72
  48.9 146.2 %copy-start.6 = (f32[512,256]{1,0:T(8,128)S(1)}, f32[512,256]{1,0:T(8,128)}, u32[]{:S(2)}) copy-start(f32[512,256]{1,0:T(8,128)} %reduce-scatter.9.cloned.1.call-done) | copy-start | bytes 1572868
  192.9 3.3 %copy-start.5 = (f32[256,512]{1,0:T(8,128)S(1)}, f32[256,512]{1,0:T(8,128)}, u32[]{:S(2)}) copy-start(f32[256,512]{1,0:T(8,128)} %reduce-scatter.11.cloned.1.call-done) | copy-start | bytes 1572868
  195.0 52.7 %all-gather.11.cloned.1.call-start = ((), (), s32[]{:S(2)}) async-start(), calls=%async_computation.9 | async-start | bytes 1310720 | tf_op jit(solution)/shard_map/all_gather | solution.py:73
  195.1 2.3 copy-start.4
  196.1 80.4 %all-gather.13.cloned.1.call-start = ((), (), s32[]{:S(2)}) async-start(), calls=%async_computation.11 | async-start | bytes 1310720 | tf_op jit(solution)/shard_map/all_gather | solution.py:74
  196.2 2.2 copy-start.14
  196.2 3.4 %copy-start.10 = (f32[1,2048]{1,0:T(1,128)S(1)}, f32[1,2048]{1,0:T(1,128)}, u32[]{:S(2)}) copy-start(f32[1,2048]{1,0:T(1,128)} %param.16) | copy-start | bytes 24580
  196.2 3.4 %copy-start.11 = (f32[1,2048]{1,0:T(1,128)S(1)}, f32[1,2048]{1,0:T(1,128)}, u32[]{:S(2)}) copy-start(f32[1,2048]{1,0:T(1,128)} %param.17) | copy-start | bytes 24580
  196.3 18.6 %copy-start.12 = (f32[512]{0:T(512)S(1)}, f32[512]{0:T(512)}, u32[]{:S(2)}) copy-start(f32[512]{0:T(512)} %param.23) | copy-start | bytes 6148
  196.3 18.6 %copy-start.13 = (f32[512]{0:T(512)S(1)}, f32[512]{0:T(512)}, u32[]{:S(2)}) copy-start(f32[512]{0:T(512)} %param.22) | copy-start | bytes 6148
  197.3 108.2 %all-gather.7.cloned.1.call-start = ((), (), s32[]{:S(2)}) async-start(), calls=%async_computation.5 | async-start | bytes 1310720 | tf_op jit(solution)/shard_map/all_gather | solution.py:71
  232.0 75.9 %copy-start.7 = (bf16[2048,256]{1,0:T(8,128)(2,1)S(1)}, bf16[2048,256]{1,0:T(8,128)(2,1)}, u32[]{:S(2)}) copy-start(bf16[2048,256]{1,0:T(8,128)(2,1)} %all-gather.9.cloned.1.call-done) | copy-start | bytes 3145732
  305.5 3.3 %copy-start.8 = (bf16[2048,256]{1,0:T(8,128)(2,1)S(1)}, bf16[2048,256]{1,0:T(8,128)(2,1)}, u32[]{:S(2)}) copy-start(bf16[2048,256]{1,0:T(8,128)(2,1)} %all-gather.11.cloned.1.call-done) | copy-start | bytes 3145732
  307.9 1.9 copy-start.9
Sparse Core Ops, SparseCore 0:
  11.0 37.9 reduce-scatter.8
  51.9 35.1 reduce-scatter.10
  90.1 35.1 reduce-scatter.4
  128.1 35.1 reduce-scatter.6
  195.1 23.7 all-gather.8
  221.3 26.4 all-gather.10
  250.2 26.3 all-gather.12
  279.0 26.4 all-gather.6
where the time goes:
time: 318 us
  waiting for transfers between devices  225 us (71%)
  blocking collectives  58.7 us (18%)
  between operations  15 us (5%)
  other arithmetic  11.2 us (4%)
  local copies, waits for them, and re-layouts  7.37 us (2%)
    reduce_scatter x1, waiting for transfers between devices, per_device(): lax.psum_scatter(grad_value[0], 'batch', scatter_dimension=0, tiled=True)  38.1 us
    reduce_scatter x1, waiting for transfers between devices, per_device(): lax.psum_scatter(grad_query[0], 'batch', scatter_dimension=0, tiled=True)  37.1 us
    reduce_scatter x1, waiting for transfers between devices, per_device(): lax.psum_scatter(grad_mixed[0], 'batch', scatter_dimension=1, tiled=True)  36.9 us
    reduce_scatter x1, waiting for transfers between devices, per_device(): lax.psum_scatter(grad_key[0], 'batch', scatter_dimension=0, tiled=True)  36.8 us
    all_gather x1, waiting for transfers between devices, per_device(): lax.all_gather(new_query.astype(jnp.bfloat16), 'batch', axis=0, tiled=True)  28.9 us
    all_gather x1, waiting for transfers between devices, per_device(): lax.all_gather(new_mixed.astype(jnp.bfloat16), 'batch', axis=1, tiled=True)  28.8 us
    psum x1, blocking collectives, per_device(): lax.psum((jnp.sum(weight_query * weight_query, axis=1, keepdims=True), jn...  28.3 us
    all_gather x1, waiting for transfers between devices, per_device(): lax.all_gather(new_value.astype(jnp.bfloat16), 'batch', axis=0, tiled=True)  15.8 us
  transfers between devices with their start and end apart: 8, of which 7 were waited for; matrix products, arithmetic and copies ran while one was open for 3% of the time, Pallas kernels for 0%

commit v1 on v0

v1 whole, which is shorter than its diff:
```python
import functools
import math

import jax
import jax.numpy as jnp
from jax import lax
from jax.experimental import pallas as pl
from jax.experimental.pallas import tpu as pltpu
from jax.sharding import PartitionSpec as P

learn_rate = 0.4
LANES = 128


def kernel(n, m, n_x, n_y, *refs):
    grads, small_grads = refs[0:4], refs[4:6]
    weights, small_weights = refs[6:10], refs[10:12]
    copies, news = refs[12:16], refs[16:20]
    small_full, small_own = refs[20:22]
    scratch = refs[22:]
    first_in, second_in, held = scratch[0:4], scratch[4:8], scratch[8:12]
    total, own_weight = scratch[12:16], scratch[16:20]
    squares, squares_in, small_grad_in, small_weight_in = scratch[20:24]
    (
        load_sem, weight_sem,
        first_send, first_recv, second_send, second_recv,
        square_send, square_recv, square_own,
        back_send, back_recv, spread_send, spread_recv,
        small_send, small_recv, small_local,
    ) = scratch[24:]
    rate = n ** (-0.5)

    me = lax.axis_index("batch")
    col = lax.axis_index("cols")
    y, x = me // n_x, lax.rem(me, n_x)

    def spot(half, d_first, d_second):
        if half == 0:
            return lax.rem(y + d_second, n_y) * n_x + lax.rem(x + d_first, n_x)
        return lax.rem(y + d_first, n_y) * n_x + lax.rem(x + d_second, n_x)

    def extents(half):
        return (n_x, n_y) if half == 0 else (n_y, n_x)

    def piece(a, ref, chunk, half):
        rows, columns = total[a].shape
        depth = rows // 2
        if a < 3:
            start = pl.multiple_of(chunk * rows + half * depth, depth)
            return ref.at[pl.ds(start, depth), :]
        start = pl.multiple_of(chunk * columns, columns)
        return ref.at[pl.ds(half * depth, depth), pl.ds(start, columns)]

    loads, weight_loads = {}, []
    for a in range(4):
        for half in range(2):
            for d in range(extents(half)[1]):
                loads[a, half, d] = pltpu.make_async_copy(
                    piece(a, grads[a].at[0], spot(half, 0, d), half),
                    held[a].at[half, d],
                    load_sem.at[a, half, d],
                )
        weight_loads.append(pltpu.make_async_copy(weights[a], own_weight[a], weight_sem.at[a]))
    small_loads = []
    for i in range(2):
        small_loads.append(pltpu.make_async_copy(small_grads[i], small_grad_in.at[me, i], small_local.at[i]))
        small_loads.append(pltpu.make_async_copy(small_weights[i], small_weight_in.at[me, i], small_local.at[2 + i]))

    barrier = pltpu.get_barrier_semaphore()
    for d in range(1, n):
        pl.semaphore_signal(barrier, inc=1, device_id={"batch": lax.rem(me + d, n)})
    for d in range(1, m):
        pl.semaphore_signal(barrier, inc=1, device_id={"cols": lax.rem(col + d, m)})
    for copy in weight_loads:
        copy.start()
    for copy in loads.values():
        copy.start()
    for copy in small_loads:
        copy.start()
    pl.semaphore_wait(barrier, n - 1 + m - 1)

    first = {}
    for a in range(4):
        for d_second in range(max(n_x, n_y) - 1, -1, -1):
            for half in range(2):
                n_first, n_second = extents(half)
                if d_second >= n_second:
                    continue
                for d_first in range(1, n_first):
                    copy = pltpu.make_async_remote_copy(
                        src_ref=piece(a, grads[a].at[0], spot(half, d_first, d_second), half),
                        dst_ref=first_in[a].at[half, d_first - 1, d_second],
                        send_sem=first_send.at[a, half, d_first - 1, d_second],
                        recv_sem=first_recv.at[a, half, d_first - 1, d_second],
                        device_id={"batch": spot(half, d_first, 0)},
                    )
                    copy.start()
                    first[a, half, d_first, d_second] = copy
        if a == 0:
            small = []
            for d in range(1, n):
                for i in range(2):
                    for k, (source, target) in enumerate(
                        ((small_grads[i], small_grad_in), (small_weights[i], small_weight_in))
                    ):
                        copy = pltpu.make_async_remote_copy(
                            src_ref=source,
                            dst_ref=target.at[me, i],
                            send_sem=small_send.at[d - 1, i, k],
                            recv_sem=small_recv.at[d - 1, i, k],
                            device_id={"batch": lax.rem(me + d, n)},
                        )
                        copy.start()
                        small.append(copy)

    def row_squares(a, value):
        value = value * value
        if a == 3:
            return jnp.sum(value, axis=0, keepdims=True)
        folded = value[:, :LANES]
        for start in range(LANES, value.shape[1], LANES):
            folded = folded + value[:, start : start + LANES]
        return jnp.sum(folded.T, axis=0, keepdims=True)

    for a in range(4):
        weight_loads[a].wait()
        squares[a, 0:1] = row_squares(a, own_weight[a][...])

    second = {}

    def add_first(a):
        for d_second in range(max(n_x, n_y) - 1, -1, -1):
            for half in range(2):
                n_first, n_second = extents(half)
                if d_second >= n_second:
                    continue
                loads[a, half, d_second].wait()
                value = held[a][half, d_second]
                for d_first in range(1, n_first):
                    first[a, half, d_first, d_second].wait_recv()
                    value = value + first_in[a][half, d_first - 1, d_second]
                held[a][half, d_second] = value
                if d_second > 0:
                    copy = pltpu.make_async_remote_copy(
                        src_ref=held[a].at[half, d_second],
                        dst_ref=second_in[a].at[half, d_second - 1],
                        send_sem=second_send.at[a, half, d_second - 1],
                        recv_sem=second_recv.at[a, half, d_second - 1],
                        device_id={"batch": spot(half, 0, d_second)},
                    )
                    copy.start()
                    second[a, half, d_second] = copy

    exchange = {}

    def add_second(a):
        depth = total[a].shape[0] // 2
        for half in range(2):
            value = held[a][half, 0]
            for d_second in range(1, extents(half)[1]):
                second[a, half, d_second].wait_recv()
                value = value + second_in[a][half, d_second - 1]
            total[a][half * depth : (half + 1) * depth] = value * rate
        squares[a, 1:2] = row_squares(a, total[a][...])
        own = pltpu.make_async_copy(squares.at[a], squares_in.at[a, col], square_own.at[a])
        exchange[a] = [own]
        for d in range(1, m):
            copy = pltpu.make_async_remote_copy(
                src_ref=squares.at[a],
                dst_ref=squares_in.at[a, col],
                send_sem=square_send.at[a, d - 1],
                recv_sem=square_recv.at[a, d - 1],
                device_id={"cols": lax.rem(col + d, m)},
            )
            copy.start()
            exchange[a].append(copy)
        own.start()

    back, spread = {}, {}

    def send_spread(a, half, d_second):
        n_first, n_second = extents(half)
        slab = piece(a, copies[a], spot(half, 0, n_second - d_second), half)
        for d_first in range(1, n_first):
            copy = pltpu.make_async_remote_copy(
                src_ref=slab,
                dst_ref=slab,
                send_sem=spread_send.at[a, half, d_first - 1, d_second],
                recv_sem=spread_recv.at[a, half, d_first - 1, d_second],
                device_id={"batch": spot(half, d_first, 0)},
            )
            copy.start()
            spread[a, half, d_first, d_second] = copy

    def update(a):
        exchange[a][0].wait()
        for copy in exchange[a][1:]:
            copy.wait_recv()
        both = squares_in[a, 0]
        for d in range(1, m):
            both = both + squares_in[a, d]
        ratio = learn_rate * (jnp.sqrt(both[0:1]) * lax.rsqrt(both[1:2] + 1e-06))
        rows, columns = total[a].shape
        if a < 3:
            ratio = jnp.broadcast_to(ratio, (LANES, rows)).T
            for start in range(0, columns, LANES):
                block = slice(start, start + LANES)
                news[a][:, block] = own_weight[a][:, block] - total[a][:, block] * ratio
        else:
            news[a][...] = own_weight[a][...] - total[a][...] * ratio
        depth = rows // 2
        for half in range(2):
            piece(a, copies[a], me, half)[...] = news[a][half * depth : (half + 1) * depth].astype(jnp.bfloat16)
        for half in range(2):
            slab = piece(a, copies[a], me, half)
            for d_second in range(1, extents(half)[1]):
                copy = pltpu.make_async_remote_copy(
                    src_ref=slab,
                    dst_ref=slab,
                    send_sem=back_send.at[a, half, d_second - 1],
                    recv_sem=back_recv.at[a, half, d_second - 1],
                    device_id={"batch": spot(half, 0, d_second)},
                )
                copy.start()
                back[a, half, d_second] = copy
            send_spread(a, half, 0)

    def pass_on(a):
        for half in range(2):
            for d_second in range(1, extents(half)[1]):
                back[a, half, d_second].wait_recv()
                send_spread(a, half, d_second)

    add_first(0)
    for copy in small_loads:
        copy.wait()
    for copy in small:
        copy.wait()
    width = small_weight_in.shape[-1]
    for i in range(2):
        value = small_grad_in[0, i]
        for j in range(1, n):
            value = value + small_grad_in[j, i]
        value = value * rate
        for j in range(n):
            small_full[i, j] = small_weight_in[j, i] - learn_rate * value[:, j * width : (j + 1) * width]
        small_own[i] = small_full[i, me]
    for a in range(1, 4):
        add_first(a)
    add_second(0)
    add_second(1)
    update(0)
    add_second(2)
    update(1)
    add_second(3)
    update(2)
    pass_on(0)
    update(3)
    for a in range(1, 4):
        pass_on(a)
    for copies_sent in (first, second, back, spread):
        for copy in copies_sent.values():
            copy.wait_send()
    for a in range(4):
        for copy in exchange[a][1:]:
            copy.wait_send()
    for copy in spread.values():
        copy.wait_recv()


def solution(mesh):
    n, m = mesh.shape["batch"], mesh.shape["cols"]
    n_x = math.isqrt(n)
    if n_x * n_x != n:
        n_x = n
    n_y = n // n_x
    most = max(n_x, n_y)

    def per_device(*args):
        grads, small_grads, weights, small_weights = args[0:4], args[4:6], args[6:10], args[10:12]
        width = small_weights[0].shape[0]
        blocks = [w.shape for w in weights]
        slices = blocks[0][0]
        slabs = [(b[0] // 2, b[1]) for b in blocks]
        f32, bf16 = jnp.float32, jnp.bfloat16
        DMA = pltpu.SemaphoreType.DMA
        hops = max(most - 1, 1)
        anywhere = pl.BlockSpec(memory_space=pl.ANY)
        vmem = pl.BlockSpec(memory_space=pltpu.VMEM)
        out_shape = (
            [jax.ShapeDtypeStruct(g.shape[1:], bf16) for g in grads]
            + [jax.ShapeDtypeStruct(b, f32) for b in blocks]
            + [jax.ShapeDtypeStruct((2, n, 1, width), f32), jax.ShapeDtypeStruct((2, 1, width), f32)]
        )
        results = pl.pallas_call(
            functools.partial(kernel, n, m, n_x, n_y),
            out_shape=out_shape,
            in_specs=[anywhere] * 12,
            out_specs=[vmem] * 10,
            scratch_shapes=(
                [pltpu.VMEM((2, hops, most) + s, f32) for s in slabs]
                + [pltpu.VMEM((2, hops) + s, f32) for s in slabs]
                + [pltpu.VMEM((2, most) + s, f32) for s in slabs]
                + [pltpu.VMEM(b, f32) for b in blocks]
                + [pltpu.VMEM(b, f32) for b in blocks]
                + [
                    pltpu.VMEM((4, 2, slices), f32),
                    pltpu.VMEM((4, m, 2, slices), f32),
                    pltpu.VMEM((n, 2, 1, n * width), f32),
                    pltpu.VMEM((n, 2, 1, width), f32),
                    DMA((4, 2, most)),
                    DMA((4,)),
                    DMA((4, 2, hops, most)),
                    DMA((4, 2, hops, most)),
                    DMA((4, 2, hops)),
                    DMA((4, 2, hops)),
                    DMA((4, m)),
                    DMA((4, m)),
                    DMA((4,)),
                    DMA((4, 2, hops)),
                    DMA((4, 2, hops)),
                    DMA((4, 2, hops, most)),
                    DMA((4, 2, hops, most)),
                    DMA((n, 2, 2)),
                    DMA((n, 2, 2)),
                    DMA((4,)),
                ]
            ),
            compiler_params=pltpu.CompilerParams(
                collective_id=0, has_side_effects=True, vmem_limit_bytes=40 * 2**20
            ),
        )(*grads, *small_grads, *weights, *[w.reshape(1, -1) for w in small_weights])
        full, own = results[8], results[9]
        small_copies = [full[i].reshape(-1).astype(bf16) for i in range(2)]
        small_news = [own[i].reshape(-1) for i in range(2)]
        return tuple(results[0:4]) + tuple(small_copies) + tuple(results[4:8]) + tuple(small_news)

    in_specs = (
        (P("batch", None, "cols"),) * 3
        + (P("batch", "cols", None),)
        + (P("batch", None),) * 2
        + (P("batch", "cols"),) * 3
        + (P("cols", "batch"),)
        + (P("batch"),) * 2
    )
    out_specs = (
        (P(None, "cols"),) * 3
        + (P("cols", None),)
        + (P(),) * 2
        + (P("batch", "cols"),) * 3
        + (P("cols", "batch"),)
        + (P("batch"),) * 2
    )
    return jax.shard_map(per_device, mesh=mesh, in_specs=in_specs, out_specs=out_specs, check_vma=False)
```

time: 318 us -> 132 us (0.42)
  waiting for transfers between devices: 225 us -> 0 us
  Pallas kernels: 0 us -> 112 us
  blocking collectives: 58.7 us -> 0 us
  between operations: 15 us -> 0.69 us
  local copies, waits for them, and re-layouts: 7.37 us -> 19 us
  other arithmetic: 11.2 us -> 0.01 us
    reduce_scatter x4 -> x0, waiting for transfers between devices: 149 us -> none  [the longest x1 38.1 us: per_device(): lax.psum_scatter(grad_value[0], 'batch', scatter_dimension=0, tiled=True)]
    pallas_call x0 -> x1, Pallas kernels: none -> 112 us  [per_device(): pl.pallas_call(functools.partial(kernel, n, m, n_x, n_y), out_shape=out_s...]
    all_gather x4 -> x0, waiting for transfers between devices: 73.5 us -> none  [the longest x1 28.9 us: per_device(): lax.all_gather(new_query.astype(jnp.bfloat16), 'batch', axis=0, tiled=True)]
    psum x1 -> x0, blocking collectives: 28.3 us -> none  [per_device(): lax.psum((jnp.sum(weight_query * weight_query, axis=1, keepdims=True), jn...]
    unnamed x1 -> x0, blocking collectives: 15.2 us -> none
    all_gather x2 -> x0, blocking collectives: 15.2 us -> none  [the longest x1 8.08 us: per_device(): lax.all_gather(new_norm.astype(jnp.bfloat16), 'batch', axis=0, tiled=True)]
    unnamed x39 -> x30, local copies, waits for them, and re-layouts: 7.37 us -> 18.3 us
    convert_element_type x5 -> x0, other arithmetic: 5.8 us -> none  [the longest x1 2.11 us: per_device(): new_key.astype(jnp.bfloat16)]
  transfers between devices with their start and end apart: 8 -> 0, of which waited for: 7 -> 0; matrix products, arithmetic and copies ran while one was open for 3% -> 0% of each run, Pallas kernels for 0% -> 0%
where the time goes in v1:
time: 132 us; the launch traced here: 131 us
  Pallas kernels  112 us (85%)
  local copies, waits for them, and re-layouts  19 us (14%)
    pallas_call x1, Pallas kernels, per_device(): pl.pallas_call(functools.partial(kernel, n, m, n_x, n_y), out_shape=out_s...  112 us
    unnamed x30, local copies, waits for them, and re-layouts  18.3 us

profile of v1, /device:TPU:0, one launch (start us, length us, event | category | flops | bytes accessed | tf_op | source)
XLA Modules:
  0.0 131.2 jit_solution(1152291132006630920)
XLA Ops:
  0.6 0.0 copy-start
  0.7 1.6 %copy-done = f32[1,2048,256]{2,1,0:T(8,128)S(1)} copy-done((f32[1,2048,256]{2,1,0:T(8,128)S(1)}, f32[1,2048,256]{2,1,0:T(8,128)}, u32[]{:S(2)}) %copy-start) | copy-done | bytes 2097176
  2.2 0.0 copy-start.1
  2.2 1.6 %copy-done.1 = f32[1,2048,256]{2,1,0:T(8,128)S(1)} copy-done((f32[1,2048,256]{2,1,0:T(8,128)S(1)}, f32[1,2048,256]{2,1,0:T(8,128)}, u32[]{:S(2)}) %copy-start.1) | copy-done | bytes 2097176
  3.8 1.0 copy-done.2
  4.9 1.0 copy-done.3
  5.9 1.0 copy-done.4
  7.0 1.0 copy-done.5
  8.0 0.7 copy-done.6
  8.7 0.7 copy-done.7
  9.4 0.7 copy-done.8
  10.1 0.7 copy-done.9
  10.8 111.5 %shard_map.211 = (bf16[2048,256]{1,0:T(8,128)(2,1)S(1)}, bf16[2048,256]{1,0:T(8,128)(2,1)S(1)}, bf16[2048,256]{1,0:T(8,128)(2,1)S(1)}, bf16[256,2048]{1,0:T(8,12...) custom-call(f32[1,2048,256]{2,1,0:T(8,128)S(1)} %copy-done, ...), custom_call_target="tpu_custom_call" | custom-call | tf_op jit(solution)/shard_map/pallas_call | solution.py:295
  122.4 0.6 copy.24
  123.0 0.6 copy.25
  123.6 0.6 fusion
  124.1 1.0 copy.34
  125.1 1.0 copy.35
  126.1 1.0 copy.36
  127.1 1.0 copy.37
  128.0 0.8 copy.38
  128.8 0.8 copy.39
  129.6 0.8 copy.40
  130.4 0.8 copy.41
  (10 shorter events, 0.1 us)
Async XLA Ops:
  0.6 1.6 %copy-start = (f32[1,2048,256]{2,1,0:T(8,128)S(1)}, f32[1,2048,256]{2,1,0:T(8,128)}, u32[]{:S(2)}) copy-start(f32[1,2048,256]{2,1,0:T(8,128)} %refs_0_.1) | copy-start | bytes 6291460
  2.2 1.6 %copy-start.1 = (f32[1,2048,256]{2,1,0:T(8,128)S(1)}, f32[1,2048,256]{2,1,0:T(8,128)}, u32[]{:S(2)}) copy-start(f32[1,2048,256]{2,1,0:T(8,128)} %refs_1_.1) | copy-start | bytes 6291460
  3.8 1.0 copy-start.2
  4.9 1.0 copy-start.3
  5.9 1.0 copy-start.4
  7.0 1.0 copy-start.5
  8.0 0.7 copy-start.6
  8.7 0.7 copy-start.7
  9.4 0.7 copy-start.8
  10.1 0.7 copy-start.9

commit v2 on v1

--- a/solution.py
+++ b/solution.py
@@ -268,6 +268,27 @@
         copy.wait_recv()
 
 
+def finish(n, *refs):
+    results, full, own = refs[0:8], refs[8], refs[9]
+    outs, small_copies, small_news = refs[10:18], refs[18:20], refs[20:22]
+    copy_rows, new_rows, sem, small_sem = refs[22:24], refs[24:26], refs[26], refs[27]
+    moves = [pltpu.make_async_copy(results[i], outs[i], sem.at[i]) for i in range(8)]
+    for move in moves:
+        move.start()
+    width = full.shape[-1]
+    for i in range(2):
+        for j in range(n):
+            copy_rows[i][j * width : (j + 1) * width] = full[i, j, 0].astype(jnp.bfloat16)
+        new_rows[i][...] = own[i, 0]
+    for i in range(2):
+        moves.append(pltpu.make_async_copy(copy_rows[i], small_copies[i], small_sem.at[i]))
+        moves.append(pltpu.make_async_copy(new_rows[i], small_news[i], small_sem.at[2 + i]))
+    for move in moves[8:]:
+        move.start()
+    for move in moves:
+        move.wait()
+
+
 def solution(mesh):
     n, m = mesh.shape["batch"], mesh.shape["cols"]
     n_x = math.isqrt(n)
@@ -277,15 +298,15 @@
     most = max(n_x, n_y)
 
     def per_device(*args):
-        grads, small_grads, weights, small_weights = args[0:4], args[4:6], args[6:10], args[10:12]
-        width = small_weights[0].shape[0]
+        args = args[:10] + tuple(w.reshape(1, -1) for w in args[10:])
+        grads, weights, width = args[0:4], args[6:10], args[10].shape[1]
         blocks = [w.shape for w in weights]
         slices = blocks[0][0]
         slabs = [(b[0] // 2, b[1]) for b in blocks]
         f32, bf16 = jnp.float32, jnp.bfloat16
         DMA = pltpu.SemaphoreType.DMA
         hops = max(most - 1, 1)
-        anywhere = pl.BlockSpec(memory_space=pl.ANY)
+        hbm = pl.BlockSpec(memory_space=pltpu.HBM)
         vmem = pl.BlockSpec(memory_space=pltpu.VMEM)
         out_shape = (
             [jax.ShapeDtypeStruct(g.shape[1:], bf16) for g in grads]
@@ -294,8 +315,8 @@
         )
         results = pl.pallas_call(
             functools.partial(kernel, n, m, n_x, n_y),
-            out_shape=out_shape,
-            in_specs=[anywhere] * 12,
+            out_shape=[pltpu.VMEM(o.shape, o.dtype) for o in out_shape],
+            in_specs=[hbm] * 12,
             out_specs=[vmem] * 10,
             scratch_shapes=(
                 [pltpu.VMEM((2, hops, most) + s, f32) for s in slabs]
@@ -329,11 +350,20 @@
             compiler_params=pltpu.CompilerParams(
                 collective_id=0, has_side_effects=True, vmem_limit_bytes=40 * 2**20
             ),
-        )(*grads, *small_grads, *weights, *[w.reshape(1, -1) for w in small_weights])
-        full, own = results[8], results[9]
-        small_copies = [full[i].reshape(-1).astype(bf16) for i in range(2)]
-        small_news = [own[i].reshape(-1) for i in range(2)]
-        return tuple(results[0:4]) + tuple(small_copies) + tuple(results[4:8]) + tuple(small_news)
+        )(*[pltpu.with_memory_space_constraint(v, pltpu.HBM) for v in args])
+        done = pl.pallas_call(
+            functools.partial(finish, n),
+            out_shape=out_shape[:8]
+            + [jax.ShapeDtypeStruct((n * width,), bf16)] * 2
+            + [jax.ShapeDtypeStruct((width,), f32)] * 2,
+            in_specs=[vmem] * 10,
+            out_specs=[hbm] * 12,
+            scratch_shapes=[pltpu.VMEM((n * width,), bf16)] * 2
+            + [pltpu.VMEM((width,), f32)] * 2
+            + [DMA((8,)), DMA((4,))],
+            compiler_params=pltpu.CompilerParams(vmem_limit_bytes=2**20),
+        )(*results)
+        return tuple(done[0:4]) + tuple(done[8:10]) + tuple(done[4:8]) + tuple(done[10:12])
 
     in_specs = (
         (P("batch", None, "cols"),) * 3

time: 132 us -> 115 us (0.87)
  local copies, waits for them, and re-layouts: 19 us -> 0 us
  Pallas kernels: 112 us -> 115 us
    unnamed x30 -> x0, local copies, waits for them, and re-layouts: 18.3 us -> none
    pallas_call x1 -> x2, Pallas kernels: 112 us -> 115 us  [the longest x1 112 us: per_device(): pl.pallas_call(functools.partial(kernel, n, m, n_x, n_y), out_shape=[pltp...]
where the time goes in v2:
time: 115 us
  Pallas kernels  115 us (100%)
    pallas_call x1, Pallas kernels, per_device(): pl.pallas_call(functools.partial(kernel, n, m, n_x, n_y), out_shape=[pltp...  112 us
    pallas_call x1, Pallas kernels, per_device(): pl.pallas_call(functools.partial(finish, n), out_shape=out_shape[:8] + [j...  2.78 us

profile of v2, /device:TPU:0, one launch (start us, length us, event | category | flops | bytes accessed | tf_op | source)
XLA Modules:
  0.0 115.3 jit_solution(10763239136627848823)
XLA Ops:
  0.6 111.8 %shard_map.211 = (bf16[2048,256]{1,0:T(8,128)(2,1)S(1)}, bf16[2048,256]{1,0:T(8,128)(2,1)S(1)}, bf16[2048,256]{1,0:T(8,128)(2,1)S(1)}, bf16[256,2048]{1,0:T(8,12...) custom-call(f32[1,2048,256]{2,1,0:T(8,128)} %refs_0_.1, ...), custom_call_target="tpu_custom_call" | custom-call | tf_op jit(solution)/shard_map/pallas_call | solution.py:316
  112.5 2.8 %shard_map.212 = (bf16[2048,256]{1,0:T(8,128)(2,1)}, bf16[2048,256]{1,0:T(8,128)(2,1)}, bf16[2048,256]{1,0:T(8,128)(2,1)}, bf16[256,2048]{1,0:T(8,128)(2,1)}, f3...) custom-call(bf16[2048,256]{1,0:T(8,128)(2,1)S(1)} %get-tuple-element, ...), custom_call_target="tpu_custom_call" | custom-call | tf_op jit(solution)/shard_map/pallas_call | solution.py:354

commit v3 on v2

--- a/solution.py
+++ b/solution.py
@@ -10,6 +10,10 @@
 
 learn_rate = 0.4
 LANES = 128
+ORDER = (
+    ("F0", "F1", "S", "W0", "W1", "W2", "W3", "A0", "F2", "A1", "F3", "N", "B0")
+    + ("A2", "B1", "U0", "A3", "B2", "U1", "P0", "B3", "U2", "P1", "U3", "P2", "P3")
+)
 
 
 def kernel(n, m, n_x, n_y, *refs):
@@ -20,14 +24,14 @@
     scratch = refs[22:]
     first_in, second_in, held = scratch[0:4], scratch[4:8], scratch[8:12]
     total, own_weight = scratch[12:16], scratch[16:20]
-    squares, squares_in, small_grad_in, small_weight_in = scratch[20:24]
+    squares, squares_in, small_in = scratch[20:23]
     (
         load_sem, weight_sem,
         first_send, first_recv, second_send, second_recv,
         square_send, square_recv, square_own,
         back_send, back_recv, spread_send, spread_recv,
         small_send, small_recv, small_local,
-    ) = scratch[24:]
+    ) = scratch[23:]
     rate = n ** (-0.5)
 
     me = lax.axis_index("batch")
@@ -61,26 +65,33 @@
                     load_sem.at[a, half, d],
                 )
         weight_loads.append(pltpu.make_async_copy(weights[a], own_weight[a], weight_sem.at[a]))
-    small_loads = []
+    small_loads, width = [], small_weights[0].shape[1]
     for i in range(2):
-        small_loads.append(pltpu.make_async_copy(small_grads[i], small_grad_in.at[me, i], small_local.at[i]))
-        small_loads.append(pltpu.make_async_copy(small_weights[i], small_weight_in.at[me, i], small_local.at[2 + i]))
+        small_loads.append(
+            pltpu.make_async_copy(small_grads[i], small_in.at[me, :, pl.ds(i * n * width, n * width)], small_local.at[i])
+        )
+        small_loads.append(
+            pltpu.make_async_copy(
+                small_weights[i], small_in.at[me, :, pl.ds((2 * n + i) * width, width)], small_local.at[2 + i]
+            )
+        )
 
     barrier = pltpu.get_barrier_semaphore()
     for d in range(1, n):
         pl.semaphore_signal(barrier, inc=1, device_id={"batch": lax.rem(me + d, n)})
     for d in range(1, m):
         pl.semaphore_signal(barrier, inc=1, device_id={"cols": lax.rem(col + d, m)})
+    for copy in small_loads:
+        copy.start()
     for copy in weight_loads:
         copy.start()
     for copy in loads.values():
         copy.start()
-    for copy in small_loads:
-        copy.start()
     pl.semaphore_wait(barrier, n - 1 + m - 1)
 
-    first = {}
-    for a in range(4):
+    first, small = {}, []
+
+    def send_first(a):
         for d_second in range(max(n_x, n_y) - 1, -1, -1):
             for half in range(2):
                 n_first, n_second = extents(half)
@@ -96,22 +107,20 @@
                     )
                     copy.start()
                     first[a, half, d_first, d_second] = copy
-        if a == 0:
-            small = []
-            for d in range(1, n):
-                for i in range(2):
-                    for k, (source, target) in enumerate(
-                        ((small_grads[i], small_grad_in), (small_weights[i], small_weight_in))
-                    ):
-                        copy = pltpu.make_async_remote_copy(
-                            src_ref=source,
-                            dst_ref=target.at[me, i],
-                            send_sem=small_send.at[d - 1, i, k],
-                            recv_sem=small_recv.at[d - 1, i, k],
-                            device_id={"batch": lax.rem(me + d, n)},
-                        )
-                        copy.start()
-                        small.append(copy)
+
+    def send_small():
+        for copy in small_loads:
+            copy.wait()
+        for d in range(1, n):
+            copy = pltpu.make_async_remote_copy(
+                src_ref=small_in.at[me],
+                dst_ref=small_in.at[me],
+                send_sem=small_send.at[d - 1],
+                recv_sem=small_recv.at[d - 1],
+                device_id={"batch": lax.rem(me + d, n)},
+            )
+            copy.start()
+            small.append(copy)
 
     def row_squares(a, value):
         value = value * value
@@ -122,7 +131,7 @@
             folded = folded + value[:, start : start + LANES]
         return jnp.sum(folded.T, axis=0, keepdims=True)
 
-    for a in range(4):
+    def weigh(a):
         weight_loads[a].wait()
         squares[a, 0:1] = row_squares(a, own_weight[a][...])
 
@@ -231,33 +240,24 @@
                 back[a, half, d_second].wait_recv()
                 send_spread(a, half, d_second)
 
-    add_first(0)
-    for copy in small_loads:
-        copy.wait()
-    for copy in small:
-        copy.wait()
-    width = small_weight_in.shape[-1]
-    for i in range(2):
-        value = small_grad_in[0, i]
-        for j in range(1, n):
-            value = value + small_grad_in[j, i]
-        value = value * rate
-        for j in range(n):
-            small_full[i, j] = small_weight_in[j, i] - learn_rate * value[:, j * width : (j + 1) * width]
-        small_own[i] = small_full[i, me]
-    for a in range(1, 4):
-        add_first(a)
-    add_second(0)
-    add_second(1)
-    update(0)
-    add_second(2)
-    update(1)
-    add_second(3)
-    update(2)
-    pass_on(0)
-    update(3)
-    for a in range(1, 4):
-        pass_on(a)
+    def update_small():
+        for copy in small:
+            copy.wait()
+        for i in range(2):
+            value = small_in[0, :, i * n * width : (i + 1) * n * width]
+            for j in range(1, n):
+                value = value + small_in[j, :, i * n * width : (i + 1) * n * width]
+            value = value * rate
+            for j in range(n):
+                weight = small_in[j, :, (2 * n + i) * width : (2 * n + i + 1) * width]
+                small_full[i, j] = weight - learn_rate * value[:, j * width : (j + 1) * width]
+            small_own[i] = small_full[i, me]
+
+    steps = dict(
+        F=send_first, S=send_small, W=weigh, A=add_first, N=update_small, B=add_second, U=update, P=pass_on
+    )
+    for step in ORDER:
+        steps[step[0]](*map(int, step[1:]))
     for copies_sent in (first, second, back, spread):
         for copy in copies_sent.values():
             copy.wait_send()
@@ -327,8 +327,7 @@
                 + [
                     pltpu.VMEM((4, 2, slices), f32),
                     pltpu.VMEM((4, m, 2, slices), f32),
-                    pltpu.VMEM((n, 2, 1, n * width), f32),
-                    pltpu.VMEM((n, 2, 1, width), f32),
+                    pltpu.VMEM((n, 1, 2 * (n + 1) * width), f32),
                     DMA((4, 2, most)),
                     DMA((4,)),
                     DMA((4, 2, hops, most)),
@@ -342,8 +341,8 @@
                     DMA((4, 2, hops)),
                     DMA((4, 2, hops, most)),
                     DMA((4, 2, hops, most)),
-                    DMA((n, 2, 2)),
-                    DMA((n, 2, 2)),
+                    DMA((n,)),
+                    DMA((n,)),
                     DMA((4,)),
                 ]
             ),

time: 115 us -> 115 us (level)
  no operation moved by 1% of the time
where the time goes in v3:
time: 115 us
  Pallas kernels  114 us (99%)
    pallas_call x1, Pallas kernels, per_device(): pl.pallas_call(functools.partial(kernel, n, m, n_x, n_y), out_shape=[pltp...  112 us
    pallas_call x1, Pallas kernels, per_device(): pl.pallas_call(functools.partial(finish, n), out_shape=out_shape[:8] + [j...  2.78 us

profile of v3, /device:TPU:0, one launch (start us, length us, event | category | flops | bytes accessed | tf_op | source)
XLA Modules:
  0.0 115.1 jit_solution(6842031095926527369)
XLA Ops:
  0.6 111.6 %shard_map.211 = (bf16[2048,256]{1,0:T(8,128)(2,1)S(1)}, bf16[2048,256]{1,0:T(8,128)(2,1)S(1)}, bf16[2048,256]{1,0:T(8,128)(2,1)S(1)}, bf16[256,2048]{1,0:T(8,12...) custom-call(f32[1,2048,256]{2,1,0:T(8,128)} %refs_0_.1, ...), custom_call_target="tpu_custom_call" | custom-call | tf_op jit(solution)/shard_map/pallas_call | solution.py:316
  112.3 2.8 %shard_map.212 = (bf16[2048,256]{1,0:T(8,128)(2,1)}, bf16[2048,256]{1,0:T(8,128)(2,1)}, bf16[2048,256]{1,0:T(8,128)(2,1)}, bf16[256,2048]{1,0:T(8,128)(2,1)}, f3...) custom-call(bf16[2048,256]{1,0:T(8,128)(2,1)S(1)} %get-tuple-element, ...), custom_call_target="tpu_custom_call" | custom-call | tf_op jit(solution)/shard_map/pallas_call | solution.py:353
